TPU v7x, 32 devices: a whole 2x2x4 slice. The times are simulated.
32 devices in a mesh: dp: 8 (over z, core), tp: 4 (over y, x).
Axes of the slice: x: 2, y: 2, z: 4, core: 2. Of those that a mesh axis runs over, the one named last changes fastest.
Arguments:
- master: float32 [4096, 10240], P(('dp', 'tp')), may hold values from -0.09375 to 0.09375
- grad: float32 [4096, 10240], P(('dp', 'tp')), may hold values from -0.006 to 0.006
- exp_avg: float32 [4096, 10240], P(('dp', 'tp')), may hold values from -0.006 to 0.006
- exp_avg_sq: float32 [4096, 10240], P(('dp', 'tp')), may hold values from 1e-08 to 1e-05
Outputs:
- new_master: float32 [4096, 10240], P(('dp', 'tp'))
- new_avg: float32 [4096, 10240], P(('dp', 'tp'))
- new_avg_sq: float32 [4096, 10240], P(('dp', 'tp'))
- engine_qkv: bfloat16 [4096, 10240], P(None, 'tp')
All inputs are finite; a program needn't handle non-finite values.
Results may differ from a plain program's by a relative error of at most 0.001.
Values may be sent and summed in bfloat16 or wider, within the bound.
A program may use at most 128 MiB of HBM per device.

v0:
```python
import jax
import jax.numpy as jnp
from jax import lax
from jax.sharding import PartitionSpec as P

QH = 64
KVH = 8
HS = 128


def joined_slices(weights, tp_count):
    rows = weights.shape[0]
    query = weights[:, : QH * HS].reshape(rows, tp_count, QH // tp_count * HS)
    keys = weights[:, QH * HS : (QH + KVH) * HS].reshape(rows, tp_count, KVH // tp_count * HS)
    values = weights[:, (QH + KVH) * HS :].reshape(rows, tp_count, KVH // tp_count * HS)
    return jnp.concatenate([query, keys, values], axis=2).reshape(rows, -1)


def body(master, grad, exp_avg, exp_avg_sq):
    corr_one = 1.0 - 0.9**10
    corr_two = 1.0 - 0.999**10
    new_avg = 0.9 * exp_avg + 0.1 * grad
    new_avg_sq = 0.999 * exp_avg_sq + 0.001 * grad * grad
    update = new_avg / corr_one / (jnp.sqrt(new_avg_sq / corr_two) + 1e-08)
    new_master = master - 0.001 * (update + 0.1 * master)
    tp_count = lax.axis_size("tp")
    ordered = joined_slices(new_master, tp_count).astype(jnp.bfloat16)
    group_rows = lax.all_to_all(ordered, "tp", split_axis=1, concat_axis=0, tiled=True)
    engine_qkv = lax.all_gather(group_rows, "dp", axis=0, tiled=True)
    return (new_master, new_avg, new_avg_sq, engine_qkv)


def solution(mesh):
    in_specs = (
        P(("dp", "tp"), None),
        P(("dp", "tp"), None),
        P(("dp", "tp"), None),
        P(("dp", "tp"), None),
    )
    out_specs = (P(("dp", "tp"), None), P(("dp", "tp"), None), P(("dp", "tp"), None), P(None, "tp"))
    return jax.shard_map(body, mesh=mesh, in_specs=in_specs, out_specs=out_specs, check_vma=False)
```

profile of v0, /device:TPU:0, one launch (start us, length us, event | category | flops | bytes accessed | tf_op | source)
XLA Modules:
  0.0 267.6 jit_solution(15748844206019149272)
XLA Ops:
  7.2 0.0 all-gather.2.cloned.1.call-start
  7.2 14.4 %fusion.1 = (bf16[128,10240]{1,0:T(8,128)(2,1)S(1)}, f32[128,10240]{1,0:T(8,128)}, f32[128,10240]{1,0:T(8,128)}, f32[128,10240]{1,0:T(8,128)}) fusion(f32[128,10240]{1,0:T(8,128)} %param.4, f32[128,10240]{1,0:T(8,128)} %param.5, f32[128,10240]{1,0:T(8,128)} %param.6, f32[128,10240]{1,0:T(8,128)} %param.7), kind=kLoop, calls=%fused_computation.8 | loop fusion | flops 20971520 | bytes 39321600 | tf_op jit(solution)/shard_map/convert.8
  21.6 0.1 slice.15
  21.8 0.1 copy.17
  22.0 0.2 pad_maximum_fusion
  22.2 36.1 %all_to_all.16 = bf16[128,4,2560]{2,0,1:T(8,128)(2,1)} all-to-all(bf16[128,4,2560]{2,0,1:T(8,128)(2,1)S(1)} %pad_maximum_fusion), channel_id=1, replica_groups=mesh['dp'=8,'tp'=4] {'tp'}, dimensions={1} | all-to-all | bytes 5242880 | tf_op jit(solution)/shard_map/all_to_all | solution.py:28
  58.3 0.0 all-gather.2.cloned.1.call-update
  58.3 185.3 %all-gather.2.cloned.1.call-done = bf16[4096,2560]{1,0:T(8,128)(2,1)} async-done(((bf16[512,2560]{1,0:T(8,128)(2,1)}), bf16[4096,2560]{1,0:T(8,128)(2,1)}) %all-gather.2.cloned.1.call-update) | async-done | bytes 20971536 | tf_op jit(solution)/shard_map/all_gather | solution.py:29
  243.6 17.1 %copy.19 = bf16[4096,2560]{1,0:T(8,128)(2,1)} copy(bf16[4096,2560]{1,0:T(8,128)(2,1)} %all-gather.2.cloned.1.call-done) | data formatting | bytes 41943040
  (2 shorter events, 0.1 us)
Async XLA Ops:
  7.2 236.5 %all-gather.2.cloned.1.call-start = ((), (), s32[]{:S(2)}) async-start(), calls=%async_computation.1 | async-start | bytes 23592960 | tf_op jit(solution)/shard_map/all_gather | solution.py:29
Sparse Core Ops, SparseCore 0:
  58.4 185.1 all-gather.1
where the time goes:
time: 268 us
  waiting for transfers between devices  185 us (69%)
  blocking collectives  36.1 us (13%)
  local copies, waits for them, and re-layouts  17.5 us (7%)
  other arithmetic  14.6 us (5%)
  between operations  14.1 us (5%)
    all_gather x1, waiting for transfers between devices, body(): engine_qkv = lax.all_gather(group_rows, 'dp', axis=0, tiled=True)  185 us
    all_to_all x1, blocking collectives, body(): lax.all_to_all(ordered, 'tp', split_axis=1, concat_axis=0, tiled=True)  36.1 us
    unnamed x1, local copies, waits for them, and re-layouts  17.1 us
    another operation x1, other arithmetic  14.4 us
  transfers between devices with their start and end apart: 1, of which 1 were waited for; matrix products, arithmetic and copies ran while one was open for 0% of the time, Pallas kernels for 0%

commit v1 on v0

v1 whole, which is shorter than its diff:
```python
import functools

import jax
import jax.numpy as jnp
from jax import lax
from jax.experimental import pallas as pl
from jax.experimental.pallas import tpu as pltpu
from jax.sharding import PartitionSpec as P

QH = 64
KVH = 8
HS = 128
CORES = 2
MESH = pl.DeviceIdType.MESH


def step_math(master, grad, exp_avg, exp_avg_sq):
    corr_one = 1.0 - 0.9**10
    corr_two = 1.0 - 0.999**10
    new_avg = 0.9 * exp_avg + 0.1 * grad
    new_avg_sq = 0.999 * exp_avg_sq + 0.001 * grad * grad
    update = new_avg / corr_one / (jnp.sqrt(new_avg_sq / corr_two) + 1e-08)
    new_master = master - 0.001 * (update + 0.1 * master)
    return new_master, new_avg, new_avg_sq


def pieces_of(tp_count):
    q, kv = QH // tp_count * HS, KVH // tp_count * HS
    return [
        [(t * q, q, 0), (QH * HS + t * kv, kv, q), ((QH + KVH) * HS + t * kv, kv, q + kv)]
        for t in range(tp_count)
    ]


def step_kernel(tp_count, m_ref, g_ref, a_ref, s_ref, nm_ref, na_ref, ns_ref, out_ref):
    for t, pieces in enumerate(pieces_of(tp_count)):
        for start, width, into in pieces:
            cols = pl.ds(start, width)
            new_master, new_avg, new_avg_sq = step_math(
                m_ref[:, cols], g_ref[:, cols], a_ref[:, cols], s_ref[:, cols]
            )
            nm_ref[:, cols] = new_master
            na_ref[:, cols] = new_avg
            ns_ref[:, cols] = new_avg_sq
            out_ref[t, :, pl.ds(into, width)] = new_master.astype(jnp.bfloat16)


def local_step(tp_count, master, grad, exp_avg, exp_avg_sq):
    rows, cols = master.shape
    tile = 16
    flat = pl.BlockSpec((tile, cols), lambda i: (i, 0))
    f32 = jax.ShapeDtypeStruct((rows, cols), jnp.float32)
    return pl.pallas_call(
        functools.partial(step_kernel, tp_count),
        grid=(rows // tile,),
        in_specs=[flat] * 4,
        out_specs=[flat] * 3 + [pl.BlockSpec((tp_count, tile, cols // tp_count), lambda i: (0, i, 0))],
        out_shape=[f32] * 3 + [jax.ShapeDtypeStruct((tp_count, rows, cols // tp_count), jnp.bfloat16)],
        compiler_params=pltpu.CompilerParams(vmem_limit_bytes=56 * 2**20),
        cost_estimate=pl.CostEstimate(flops=20 * rows * cols, bytes_accessed=30 * rows * cols, transcendentals=rows * cols),
    )(master, grad, exp_avg, exp_avg_sq)


def mix(t, j, count):
    out, bit = 0, 1
    while bit < count:
        out = out + ((t // bit) % 2 + (j // bit) % 2) % 2 * bit
        bit *= 2
    return out


def spread_kernel(dp_count, tp_count, parts, own_ref, out_ref, own_sem, flat_send, up_send, down_send, side_send, in_recv, side_recv):
    planes = dp_count // CORES
    dp, t = lax.axis_index("dp"), lax.axis_index("tp")
    z, core = dp // CORES, dp % CORES
    rows = own_ref.shape[1]
    part_rows = rows // parts
    has_up, has_down = z < planes - 1, z > 0
    units = tp_count * parts

    up = {"dp": dp + CORES}
    down = {"dp": dp - CORES}
    side = {"dp": z * CORES + 1 - core}

    barrier = pltpu.get_barrier_semaphore()
    for j in range(1, tp_count):
        pl.semaphore_signal(barrier, inc=1, device_id={"tp": mix(t, j, tp_count)}, device_id_type=MESH)
    pl.semaphore_signal(barrier, inc=1, device_id=side, device_id_type=MESH)

    @pl.when(has_up)
    def _():
        pl.semaphore_signal(barrier, inc=1, device_id=up, device_id_type=MESH)

    @pl.when(has_down)
    def _():
        pl.semaphore_signal(barrier, inc=1, device_id=down, device_id_type=MESH)

    pl.semaphore_wait(barrier, tp_count + has_up.astype(jnp.int32) + has_down.astype(jnp.int32))

    def place(plane, which_core, unit):
        source = mix(t, unit // parts, tp_count)
        block = (plane * CORES + which_core) * tp_count + source
        start = block * rows + unit % parts * part_rows
        return out_ref.at[pl.ds(pl.multiple_of(start, part_rows), part_rows), :]

    def copy(src, dst, send, recv, target):
        return pltpu.make_async_remote_copy(
            src_ref=src, dst_ref=dst, send_sem=send, recv_sem=recv, device_id=target, device_id_type=MESH
        )

    def going_up(src, plane, unit):
        return copy(src, place(plane, core, unit), up_send.at[plane, unit], in_recv.at[plane, unit], up)

    def going_down(src, plane, unit):
        return copy(src, place(plane, core, unit), down_send.at[plane, unit], in_recv.at[plane, unit], down)

    def going_side(src, plane, unit):
        return copy(src, place(plane, core, unit), side_send.at[plane, unit], side_recv.at[plane, unit], side)

    def arrived(plane, unit):
        here = place(plane, core, unit)
        copy(here, here, side_send.at[plane, unit], in_recv.at[plane, unit], side).wait_recv()

    def own_part(which, h):
        return own_ref.at[which, pl.ds(h * part_rows, part_rows), :]

    def flat_copy(j, h):
        target = mix(t, j, tp_count)
        start = ((z * CORES + core) * tp_count + t) * rows + h * part_rows
        dst = out_ref.at[pl.ds(pl.multiple_of(start, part_rows), part_rows), :]
        unit = j * parts + h
        return copy(own_part(target, h), dst, flat_send.at[unit], in_recv.at[z, unit], {"tp": target})

    def onward(src, unit):
        @pl.when(has_up)
        def _():
            going_up(src, z, unit).start()

        @pl.when(has_down)
        def _():
            going_down(src, z, unit).start()

    for h in range(parts):
        onward(own_part(t, h), h)
    for j in range(1, tp_count):
        for h in range(parts):
            flat_copy(j, h).start()
    keep = [pltpu.make_async_copy(own_part(t, h), place(z, core, h), own_sem.at[h]) for h in range(parts)]
    for h in range(parts):
        keep[h].start()
        going_side(own_part(t, h), z, h).start()

    @pl.loop(parts, units)
    def _(unit):
        arrived(z, unit)
        onward(place(z, core, unit), unit)
        going_side(place(z, core, unit), z, unit).start()

    @pl.loop(0, (planes - 1) * units)
    def _(m):
        distance, unit = m // units + 1, m % units
        below, above = z - distance, z + distance

        @pl.when(below >= 0)
        def _():
            arrived(below, unit)

            @pl.when(has_up)
            def _():
                going_up(place(below, core, unit), below, unit).start()

            going_side(place(below, core, unit), below, unit).start()

        @pl.when(above < planes)
        def _():
            arrived(above, unit)

            @pl.when(has_down)
            def _():
                going_down(place(above, core, unit), above, unit).start()

            going_side(place(above, core, unit), above, unit).start()

    for h in range(parts):
        keep[h].wait()
    for j in range(1, tp_count):
        for h in range(parts):
            flat_copy(j, h).wait_send()

    @pl.loop(0, planes * units)
    def _(m):
        plane, unit = m // units, m % units
        here = place(plane, core, unit)
        there = place(plane, 1 - core, unit)

        @pl.when((plane <= z) & has_up)
        def _():
            going_up(here, plane, unit).wait_send()

        @pl.when((plane >= z) & has_down)
        def _():
            going_down(here, plane, unit).wait_send()

        going_side(here, plane, unit).wait_send()
        copy(there, there, side_send.at[plane, unit], side_recv.at[plane, unit], side).wait_recv()


def spread(dp_count, tp_count, own):
    rows, width = own.shape[1:]
    parts = 2 if rows % 64 == 0 else 1
    planes, units = dp_count // CORES, tp_count * parts
    grid = pltpu.SemaphoreType.DMA((planes, units))
    return pl.pallas_call(
        functools.partial(spread_kernel, dp_count, tp_count, parts),
        in_specs=[pl.BlockSpec(memory_space=SRC)],
        out_specs=pl.BlockSpec(memory_space=DST),
        out_shape=jax.ShapeDtypeStruct((dp_count * tp_count * rows, width), jnp.bfloat16),
        scratch_shapes=[pltpu.SemaphoreType.DMA((parts,)), pltpu.SemaphoreType.DMA((units,))] + [grid] * 5,
        compiler_params=pltpu.CompilerParams(collective_id=0, has_side_effects=True, vmem_limit_bytes=LIMIT),
        cost_estimate=pl.CostEstimate(flops=0, bytes_accessed=2 * dp_count * tp_count * rows * width, transcendentals=0),
    )(own)


SRC = pl.ANY
DST = pl.ANY
LIMIT = 4 * 2**20


def body(dp_count, tp_count, master, grad, exp_avg, exp_avg_sq):
    new_master, new_avg, new_avg_sq, own = local_step(tp_count, master, grad, exp_avg, exp_avg_sq)
    return new_master, new_avg, new_avg_sq, spread(dp_count, tp_count, own)


def solution(mesh):
    flat = P(("dp", "tp"), None)
    return jax.shard_map(
        functools.partial(body, mesh.shape["dp"], mesh.shape["tp"]),
        mesh=mesh,
        in_specs=(flat,) * 4,
        out_specs=(flat, flat, flat, P(None, "tp")),
        check_vma=False,
    )
```

time: 268 us -> 204 us (0.76)
  Pallas kernels: 0 us -> 193 us
  waiting for transfers between devices: 185 us -> 0 us
  blocking collectives: 36.1 us -> 0 us
  other arithmetic: 14.6 us -> 0 us
  between operations: 14.1 us -> 0.64 us
  local copies, waits for them, and re-layouts: 17.5 us -> 9.28 us
    pallas_call x0 -> x2, Pallas kernels: none -> 193 us  [the longest x1 177 us: spread(): pl.pallas_call(functools.partial(spread_kernel, dp_count, tp_count, parts...]
    all_gather x1 -> x0, waiting for transfers between devices: 185 us -> none  [body(): engine_qkv = lax.all_gather(group_rows, 'dp', axis=0, tiled=True)]
    all_to_all x1 -> x0, blocking collectives: 36.1 us -> none  [body(): lax.all_to_all(ordered, 'tp', split_axis=1, concat_axis=0, tiled=True)]
    another operation x1 -> x0, other arithmetic: 14.4 us -> none
    unnamed x1 -> x3, local copies, waits for them, and re-layouts: 17.1 us -> 9.28 us
  transfers between devices with their start and end apart: 1 -> 0, of which waited for: 1 -> 0; matrix products, arithmetic and copies ran while one was open for 0% -> 0% of each run, Pallas kernels for 0% -> 0%
where the time goes in v1:
time: 204 us; the launch traced here: 203 us
  Pallas kernels  193 us (95%)
  local copies, waits for them, and re-layouts  9.28 us (5%)
    pallas_call x1, Pallas kernels, spread(): pl.pallas_call(functools.partial(spread_kernel, dp_count, tp_count, parts...  177 us
    pallas_call x1, Pallas kernels, local_step(): pl.pallas_call(functools.partial(step_kernel, tp_count), grid=(rows // ti...  16.2 us
    unnamed x3, local copies, waits for them, and re-layouts  9.28 us

profile of v1, /device:TPU:0, one launch (start us, length us, event | category | flops | bytes accessed | tf_op | source)
XLA Modules:
  0.0 203.3 jit_solution(4741791222812979794)
XLA Ops:
  0.6 16.2 %shard_map.75 = (f32[128,10240]{1,0:T(8,128)}, f32[128,10240]{1,0:T(8,128)}, f32[128,10240]{1,0:T(8,128)}, bf16[4,128,2560]{2,1,0:T(8,128)(2,1)}) custom-call(f32[128,10240]{1,0:T(8,128)} %m_ref.1, f32[128,10240]{1,0:T(8,128)} %g_ref.1, f32[128,10240]{1,0:T(8,128)} %a_ref.1, f32[128,10240]{1,0:T(8,128)} %s_ref.1), custom_call_target="tpu_custom_call" | custom-call | flops 26214400 | bytes 39321600 | tf_op jit(solution)/shard_map/pallas_call | solution.py:53
  16.8 0.0 copy-start
  16.8 1.7 copy-done
  18.5 177.2 %shard_map.76 = bf16[4096,2560]{1,0:T(8,128)(2,1)S(1)} custom-call(bf16[4,128,2560]{2,1,0:T(8,128)(2,1)S(1)} %copy-done), custom_call_target="tpu_custom_call" | custom-call | bytes 20971520 | tf_op jit(solution)/shard_map/pallas_call | solution.py:213
  195.8 7.5 %copy.9 = bf16[4096,2560]{1,0:T(8,128)(2,1)} copy(bf16[4096,2560]{1,0:T(8,128)(2,1)S(1)} %shard_map.76) | data formatting | bytes 41943040
Async XLA Ops:
  16.8 1.7 copy-start

commit v2 on v1

--- a/solution.py
+++ b/solution.py
@@ -32,7 +32,7 @@
     ]
 
 
-def step_kernel(tp_count, m_ref, g_ref, a_ref, s_ref, nm_ref, na_ref, ns_ref, out_ref):
+def step_kernel(tp_count, m_ref, g_ref, a_ref, s_ref, first_ref, nm_ref, na_ref, ns_ref, out_ref):
     for t, pieces in enumerate(pieces_of(tp_count)):
         for start, width, into in pieces:
             cols = pl.ds(start, width)
@@ -45,7 +45,7 @@
             out_ref[t, :, pl.ds(into, width)] = new_master.astype(jnp.bfloat16)
 
 
-def local_step(tp_count, master, grad, exp_avg, exp_avg_sq):
+def local_step(tp_count, master, grad, exp_avg, exp_avg_sq, first):
     rows, cols = master.shape
     tile = 16
     flat = pl.BlockSpec((tile, cols), lambda i: (i, 0))
@@ -53,12 +53,56 @@
     return pl.pallas_call(
         functools.partial(step_kernel, tp_count),
         grid=(rows // tile,),
-        in_specs=[flat] * 4,
+        in_specs=[flat] * 4 + [pl.BlockSpec(memory_space=pltpu.HBM)],
         out_specs=[flat] * 3 + [pl.BlockSpec((tp_count, tile, cols // tp_count), lambda i: (0, i, 0))],
         out_shape=[f32] * 3 + [jax.ShapeDtypeStruct((tp_count, rows, cols // tp_count), jnp.bfloat16)],
         compiler_params=pltpu.CompilerParams(vmem_limit_bytes=56 * 2**20),
         cost_estimate=pl.CostEstimate(flops=20 * rows * cols, bytes_accessed=30 * rows * cols, transcendentals=rows * cols),
-    )(master, grad, exp_avg, exp_avg_sq)
+    )(master, grad, exp_avg, exp_avg_sq, first)
+
+
+def own_kernel(tp_count, chunks, *refs):
+    sources, (out_ref, token_ref), held, sems = refs[:4], refs[4:6], refs[6:10], refs[10]
+    t = lax.axis_index("tp")
+    q, kv = QH // tp_count * HS, KVH // tp_count * HS
+    pieces = [(t * q, q, 0), (QH * HS + t * kv, kv, q), ((QH + KVH) * HS + t * kv, kv, q + kv)]
+    rows = out_ref.shape[0] // chunks
+    copies = []
+    for c in range(chunks):
+        part = pl.ds(c * rows, rows)
+        for n in range(4):
+            for k, (start, width, into) in enumerate(pieces):
+                copies.append(
+                    pltpu.make_async_copy(
+                        sources[n].at[part, pl.ds(pl.multiple_of(start, HS), width)],
+                        held[n].at[part, pl.ds(into, width)],
+                        sems.at[(c * 4 + n) * 3 + k],
+                    )
+                )
+    for cp in copies:
+        cp.start()
+    for c in range(chunks):
+        for cp in copies[c * 12 : (c + 1) * 12]:
+            cp.wait()
+        part = pl.ds(c * rows, rows)
+        out_ref[part, :] = step_math(*[ref[part, :] for ref in held])[0].astype(jnp.bfloat16)
+    token_ref[...] = jnp.zeros_like(token_ref)
+
+
+def own_slice(tp_count, *arrays):
+    rows, cols = arrays[0].shape
+    width = cols // tp_count
+    chunks = max(rows // 32, 1)
+    vmem = pl.BlockSpec(memory_space=pltpu.VMEM)
+    return pl.pallas_call(
+        functools.partial(own_kernel, tp_count, chunks),
+        in_specs=[pl.BlockSpec(memory_space=pltpu.HBM)] * 4,
+        out_specs=[vmem, vmem],
+        out_shape=[jax.ShapeDtypeStruct((rows, width), jnp.bfloat16), jax.ShapeDtypeStruct((8, 128), jnp.float32)],
+        scratch_shapes=[pltpu.VMEM((rows, width), jnp.float32)] * 4 + [pltpu.SemaphoreType.DMA((chunks * 12,))],
+        compiler_params=pltpu.CompilerParams(vmem_limit_bytes=60 * 2**20),
+        cost_estimate=pl.CostEstimate(flops=20 * rows * width, bytes_accessed=18 * rows * width, transcendentals=rows * width),
+    )(*arrays)
 
 
 def mix(t, j, count):
@@ -69,7 +113,7 @@
     return out
 
 
-def spread_kernel(dp_count, tp_count, parts, own_ref, out_ref, own_sem, flat_send, up_send, down_send, side_send, in_recv, side_recv):
+def spread_kernel(dp_count, tp_count, parts, own_ref, below_ref, above_ref, out_ref, own_sem, flat_send, up_send, down_send, side_send, in_recv, side_recv):
     planes = dp_count // CORES
     dp, t = lax.axis_index("dp"), lax.axis_index("tp")
     z, core = dp // CORES, dp % CORES
@@ -140,15 +184,34 @@
         def _():
             going_down(src, z, unit).start()
 
+    def given(ref, h):
+        return ref.at[pl.ds(h * part_rows, part_rows), :]
+
+    def keep(which, src, plane, h):
+        return pltpu.make_async_copy(src, place(plane, core, h), own_sem.at[which, h])
+
     for h in range(parts):
-        onward(own_part(t, h), h)
-    for j in range(1, tp_count):
-        for h in range(parts):
+
+        @pl.when(has_up & has_down)
+        def _():
+            going_up(given(below_ref, h), z - 1, h).start()
+            going_down(given(above_ref, h), z + 1, h).start()
+
+        for j in range(1, tp_count):
             flat_copy(j, h).start()
-    keep = [pltpu.make_async_copy(own_part(t, h), place(z, core, h), own_sem.at[h]) for h in range(parts)]
     for h in range(parts):
-        keep[h].start()
+        keep(0, own_part(t, h), z, h).start()
         going_side(own_part(t, h), z, h).start()
+
+        @pl.when(has_down)
+        def _():
+            keep(1, given(below_ref, h), z - 1, h).start()
+            going_side(given(below_ref, h), z - 1, h).start()
+
+        @pl.when(has_up)
+        def _():
+            keep(2, given(above_ref, h), z + 1, h).start()
+            going_side(given(above_ref, h), z + 1, h).start()
 
     @pl.loop(parts, units)
     def _(unit):
@@ -156,7 +219,7 @@
         onward(place(z, core, unit), unit)
         going_side(place(z, core, unit), z, unit).start()
 
-    @pl.loop(0, (planes - 1) * units)
+    @pl.loop(parts, (planes - 1) * units)
     def _(m):
         distance, unit = m // units + 1, m % units
         below, above = z - distance, z + distance
@@ -182,7 +245,16 @@
             going_side(place(above, core, unit), above, unit).start()
 
     for h in range(parts):
-        keep[h].wait()
+        keep(0, own_part(t, h), z, h).wait()
+
+        @pl.when(has_down)
+        def _():
+            keep(1, given(below_ref, h), z - 1, h).wait()
+
+        @pl.when(has_up)
+        def _():
+            keep(2, given(above_ref, h), z + 1, h).wait()
+
     for j in range(1, tp_count):
         for h in range(parts):
             flat_copy(j, h).wait_send()
@@ -193,11 +265,13 @@
         here = place(plane, core, unit)
         there = place(plane, 1 - core, unit)
 
-        @pl.when((plane <= z) & has_up)
+        early = (plane == z) & (unit < parts)
+
+        @pl.when((plane <= z) & has_up & jnp.logical_not(early))
         def _():
             going_up(here, plane, unit).wait_send()
 
-        @pl.when((plane >= z) & has_down)
+        @pl.when((plane >= z) & has_down & jnp.logical_not(early))
         def _():
             going_down(here, plane, unit).wait_send()
 
@@ -205,30 +279,29 @@
         copy(there, there, side_send.at[plane, unit], side_recv.at[plane, unit], side).wait_recv()
 
 
-def spread(dp_count, tp_count, own):
+def spread(dp_count, tp_count, own, below, above):
     rows, width = own.shape[1:]
     parts = 2 if rows % 64 == 0 else 1
     planes, units = dp_count // CORES, tp_count * parts
     grid = pltpu.SemaphoreType.DMA((planes, units))
     return pl.pallas_call(
         functools.partial(spread_kernel, dp_count, tp_count, parts),
-        in_specs=[pl.BlockSpec(memory_space=SRC)],
-        out_specs=pl.BlockSpec(memory_space=DST),
+        in_specs=[pl.BlockSpec(memory_space=pltpu.HBM)] * 3,
+        out_specs=pl.BlockSpec(memory_space=pl.ANY),
         out_shape=jax.ShapeDtypeStruct((dp_count * tp_count * rows, width), jnp.bfloat16),
-        scratch_shapes=[pltpu.SemaphoreType.DMA((parts,)), pltpu.SemaphoreType.DMA((units,))] + [grid] * 5,
-        compiler_params=pltpu.CompilerParams(collective_id=0, has_side_effects=True, vmem_limit_bytes=LIMIT),
+        scratch_shapes=[pltpu.SemaphoreType.DMA((3, parts)), pltpu.SemaphoreType.DMA((units,))] + [grid] * 5,
+        compiler_params=pltpu.CompilerParams(collective_id=0, has_side_effects=True, vmem_limit_bytes=4 * 2**20),
         cost_estimate=pl.CostEstimate(flops=0, bytes_accessed=2 * dp_count * tp_count * rows * width, transcendentals=0),
-    )(own)
-
-
-SRC = pl.ANY
-DST = pl.ANY
-LIMIT = 4 * 2**20
+    )(own, below, above)
 
 
 def body(dp_count, tp_count, master, grad, exp_avg, exp_avg_sq):
-    new_master, new_avg, new_avg_sq, own = local_step(tp_count, master, grad, exp_avg, exp_avg_sq)
-    return new_master, new_avg, new_avg_sq, spread(dp_count, tp_count, own)
+    first, token = own_slice(tp_count, master, grad, exp_avg, exp_avg_sq)
+    rise = [(i, i + CORES) for i in range(dp_count - CORES)]
+    below = lax.ppermute(first, "dp", rise)
+    above = lax.ppermute(first, "dp", [(b, a) for a, b in rise])
+    new_master, new_avg, new_avg_sq, own = local_step(tp_count, master, grad, exp_avg, exp_avg_sq, token)
+    return new_master, new_avg, new_avg_sq, spread(dp_count, tp_count, own, below, above)
 
 
 def solution(mesh):

time: 204 us -> 199 us (0.975)
  Pallas kernels: 193 us -> 182 us
  starting transfers between devices: 0 us -> 6.92 us
    pallas_call x1, Pallas kernels: 177 us -> 162 us  [spread(): pl.pallas_call(functools.partial(spread_kernel, dp_count, tp_count, parts...]
    ppermute x0 -> x2, starting transfers between devices: none -> 6.92 us  [the longest x1 5.62 us: body(): below = lax.ppermute(first, 'dp', rise)]
    pallas_call x0 -> x1, Pallas kernels: none -> 4.03 us  [own_slice(): pl.pallas_call(functools.partial(own_kernel, tp_count, chunks), in_specs=...]
  transfers between devices with their start and end apart: 0 -> 2, of which waited for: 0 -> 0; matrix products, arithmetic and copies ran while one was open for 0% -> 0% of each run, Pallas kernels for 0% -> 8%
where the time goes in v2:
time: 199 us
  Pallas kernels  182 us (91%)
  local copies, waits for them, and re-layouts  9.28 us (5%)
  starting transfers between devices  6.92 us (3%)
    pallas_call x1, Pallas kernels, spread(): pl.pallas_call(functools.partial(spread_kernel, dp_count, tp_count, parts...  162 us
    pallas_call x1, Pallas kernels, local_step(): pl.pallas_call(functools.partial(step_kernel, tp_count), grid=(rows // ti...  16.2 us
    unnamed x3, local copies, waits for them, and re-layouts  9.28 us
    ppermute x1, starting transfers between devices, body(): below = lax.ppermute(first, 'dp', rise)  5.62 us
    pallas_call x1, Pallas kernels, own_slice(): pl.pallas_call(functools.partial(own_kernel, tp_count, chunks), in_specs=...  4.03 us
  transfers between devices with their start and end apart: 2, of which 0 were waited for; matrix products, arithmetic and copies ran while one was open for 0% of the time, Pallas kernels for 8%

profile of v2, /device:TPU:0, one launch (start us, length us, event | category | flops | bytes accessed | tf_op | source)
XLA Modules:
  0.0 198.7 jit_solution(3211568845458976902)
XLA Ops:
  0.6 4.0 %shard_map.75 = (bf16[128,2560]{1,0:T(8,128)(2,1)}, f32[8,128]{1,0:T(8,128)}) custom-call(f32[128,10240]{1,0:T(8,128)} %m_ref.1, f32[128,10240]{1,0:T(8,128)} %g_ref.1, f32[128,10240]{1,0:T(8,128)} %a_ref.1, f32[128,10240]{1,0:T(8,128)} %s_ref.1), custom_call_target="tpu_custom_call" | custom-call | flops 6553600 | bytes 5898240 | tf_op jit(solution)/shard_map/pallas_call | solution.py:97
  4.7 1.3 collective-permute-start.1
  6.0 5.6 %collective-permute-start = (bf16[128,2560]{1,0:T(8,128)(2,1)}, bf16[128,2560]{1,0:T(8,128)(2,1)S(1)}, u32[]{:S(2)}, u32[]{:S(2)}) collective-permute-start(bf16[128,2560]{1,0:T(8,128)(2,1)} %get-tuple-element.15), channel_id=1, source_target_pairs={{0,8},{4,12},{8,16},{12,20},{16,24},{20,28},{1,9},{5,13},{9,17},{1... | collective-permute-start | bytes 1966088 | tf_op jit(solution)/shard_map/ppermute | solution.py:301
  11.6 16.2 %shard_map.76 = (f32[128,10240]{1,0:T(8,128)}, f32[128,10240]{1,0:T(8,128)}, f32[128,10240]{1,0:T(8,128)}, bf16[4,128,2560]{2,1,0:T(8,128)(2,1)}) custom-call(f32[128,10240]{1,0:T(8,128)} %m_ref.1, f32[128,10240]{1,0:T(8,128)} %g_ref.1, f32[128,10240]{1,0:T(8,128)} %a_ref.1, f32[128,10240]{1,0:T(8,128)} %s_ref.1, f32[8,128]{1,0:T(8,128)} %get-tuple-element.10.first_ref), custom_call_target="tpu_custom_call" | custom-call | flops 26214400 | bytes 39321600 | tf_op jit(solution)/shard_map/pallas_call | solution.py:53
  27.8 0.0 collective-permute-done.1.above_ref
  27.8 0.0 collective-permute-done.below_ref
  27.8 0.0 copy-start
  27.8 1.7 copy-done
  29.5 161.6 %shard_map.77 = bf16[4096,2560]{1,0:T(8,128)(2,1)S(1)} custom-call(bf16[4,128,2560]{2,1,0:T(8,128)(2,1)S(1)} %copy-done, bf16[128,2560]{1,0:T(8,128)(2,1)S(1)} %collective-permute-done.below_ref, bf16[128,2560]{1,0:T(8,128)(2,1)S(1)} %collective-permute-done.1.above_ref), custom_call_target="tpu_custom_call" | custom-call | bytes 20971520 | tf_op jit(solution)/shard_map/pallas_call | solution.py:287
  191.1 7.5 %copy.9 = bf16[4096,2560]{1,0:T(8,128)(2,1)} copy(bf16[4096,2560]{1,0:T(8,128)(2,1)S(1)} %shard_map.77) | data formatting | bytes 41943040
Async XLA Ops:
  4.7 23.1 %collective-permute-start.1 = (bf16[128,2560]{1,0:T(8,128)(2,1)}, bf16[128,2560]{1,0:T(8,128)(2,1)S(1)}, u32[]{:S(2)}, u32[]{:S(2)}) collective-permute-start(bf16[128,2560]{1,0:T(8,128)(2,1)} %get-tuple-element.15), channel_id=1, source_target_pairs={{8,0},{12,4},{16,8},{20,12},{24,16},{28,20},{9,1},{13,5},{17,9},{2... | collective-permute-start | bytes 1966088 | tf_op jit(solution)/shard_map/ppermute | solution.py:302
  6.0 21.8 %collective-permute-start = (bf16[128,2560]{1,0:T(8,128)(2,1)}, bf16[128,2560]{1,0:T(8,128)(2,1)S(1)}, u32[]{:S(2)}, u32[]{:S(2)}) collective-permute-start(bf16[128,2560]{1,0:T(8,128)(2,1)} %get-tuple-element.15), channel_id=1, source_target_pairs={{0,8},{4,12},{8,16},{12,20},{16,24},{20,28},{1,9},{5,13},{9,17},{1... | collective-permute-start | bytes 1966088 | tf_op jit(solution)/shard_map/ppermute | solution.py:301
  27.8 1.7 copy-start
